TPU v7x, 32 devices: a whole 2x2x4 slice. The times are simulated.
32 devices in a mesh: dp: 8 (over z, x), seq: 4 (over y, core).
Axes of the slice: x: 2, y: 2, z: 4, core: 2. Of those that a mesh axis runs over, the one named last changes fastest.
Arguments:
- queries: bfloat16 [8, 512, 2048], P('dp', 'seq'), may hold values from -5 to 5
- key_states: bfloat16 [8, 512, 2048], P('dp', 'seq'), may hold values from -5 to 5
- value_states: bfloat16 [8, 512, 2048], P('dp', 'seq'), may hold values from -6 to 6
- residual: bfloat16 [8, 512, 2048], P('dp', 'seq'), may hold values from -6 to 6
- enc_hidden: bfloat16 [8, 512, 1536], P('dp', 'seq'), may hold values from -6 to 6
- enc_gain: float32 [1536], replicated, may hold values from 0.1 to 1.9
- enc_bias: float32 [1536], replicated, may hold values from -0.5 to 0.5
- feature_target: int32 [8, 512], P('dp', 'seq'), may hold values from 0 to 511, as said below
- timestep: int32 [8], P('dp'), may hold values from 0 to 999
- gate_weight: bfloat16 [256, 2048], P('dp'), may hold values from -0.375 to 0.375
- lift_weight: bfloat16 [2048, 1024], P('dp'), may hold values from -0.125 to 0.125
- out_weight: bfloat16 [1024, 1536], P('dp'), may hold values from -0.1875 to 0.1875
Outputs:
- d_queries: bfloat16 [8, 512, 2048], P('dp', 'seq')
- d_keys: bfloat16 [8, 512, 2048], P('dp', 'seq')
- d_values: bfloat16 [8, 512, 2048], P('dp', 'seq')
- grad_gate: float32 [256, 2048], P('dp')
- grad_lift: float32 [2048, 1024], P('dp')
- grad_out: float32 [1024, 1536], P('dp')
Inputs may be any that keep to these rules, and one draw needn't show every extreme that they name: For each clip, feature_target is a permutation of its 512 token positions. The 128 encoder rows of one device of seq target at most 64 tokens held by any one device of seq, and exactly 64 for some.
All inputs are finite; a program needn't handle non-finite values.
Results may differ from a plain program's by a relative error of at most 0.02.
Values may be sent and summed in bfloat16 or wider, within the bound.
No kernel may reach another device: no remote copies, remote signals or barrier semaphores. Data moves between devices by JAX's collectives and lax.ppermute only.
A program may use at most 128 MiB of HBM per device.

v0:
```python
import functools
import math

import jax
import jax.numpy as jnp
from jax import lax
from jax.experimental import pallas as pl
from jax.experimental.pallas import tpu as pltpu
from jax.sharding import PartitionSpec as P


HD = 128
EPSILON = 1e-06
BF = jnp.bfloat16
F32 = jnp.float32


def embed_time(timestep, width):
    half_width = width // 2
    frequency = jnp.exp(
        -math.log(10000.0) * jnp.arange(half_width).astype(F32) / half_width
    )
    angles = timestep.astype(F32)[:, None] * frequency[None, :]
    return jnp.concatenate([jnp.cos(angles), jnp.sin(angles)], axis=1).astype(BF)


def nt(a, b):
    return lax.dot_general(a, b, (((1,), (1,)), ((), ())), preferred_element_type=F32)


def nn(a, b):
    return lax.dot_general(a, b, (((1,), (0,)), ((), ())), preferred_element_type=F32)


def tn(a, b):
    return lax.dot_general(a, b, (((0,), (0,)), ((), ())), preferred_element_type=F32)


def forward_body(blocks, *refs):
    packs, outs = refs[:blocks], refs[blocks:]
    keys = jnp.concatenate([p[1] for p in packs], axis=0)
    values = jnp.concatenate([p[2] for p in packs], axis=0)
    for pack, out in zip(packs, outs):
        scores = nt(pack[0], keys) * HD ** (-0.5)
        shifted = jnp.exp(scores - jnp.max(scores, axis=-1, keepdims=True))
        chances = shifted / jnp.sum(shifted, axis=-1, keepdims=True)
        out[...] = nn(chances.astype(BF), values).astype(BF)


def attention_forward(packs):
    blocks = len(packs)
    _, tokens, width = packs[0].shape
    heads = width // HD
    return pl.pallas_call(
        functools.partial(forward_body, blocks),
        grid=(heads,),
        in_specs=[pl.BlockSpec((3, tokens, HD), lambda h: (0, 0, h))] * blocks,
        out_specs=[pl.BlockSpec((tokens, HD), lambda h: (0, h))] * blocks,
        out_shape=[jax.ShapeDtypeStruct((tokens, width), BF)] * blocks,
        cost_estimate=pl.CostEstimate(
            flops=4 * heads * (blocks * tokens) ** 2 * HD,
            bytes_accessed=8 * blocks * tokens * width,
            transcendentals=heads * (blocks * tokens) ** 2,
        ),
        name="attend",
    )(*packs)


def backward_body(blocks, *refs):
    packs, grads, outs = refs[:blocks], refs[blocks : 2 * blocks], refs[2 * blocks + 1 :]
    keys = jnp.concatenate([p[1] for p in packs], axis=0)
    values = jnp.concatenate([p[2] for p in packs], axis=0)
    grad_keys = grad_values = None
    for pack, grad, out in zip(packs, grads, outs):
        query, grad_rows = pack[0], grad[...]
        scores = nt(keys, query) * HD ** (-0.5)
        shifted = jnp.exp(scores - jnp.max(scores, axis=0, keepdims=True))
        chances = shifted / jnp.sum(shifted, axis=0, keepdims=True)
        grad_chances = nt(values, grad_rows)
        add_values = nn(chances.astype(BF), grad_rows)
        inner = jnp.sum(grad_chances * chances, axis=0, keepdims=True)
        grad_scores = (chances * (grad_chances - inner) * HD ** (-0.5)).astype(BF)
        out[0] = tn(grad_scores, keys).astype(BF)
        add_keys = nn(grad_scores, query)
        grad_keys = add_keys if grad_keys is None else grad_keys + add_keys
        grad_values = add_values if grad_values is None else grad_values + add_values
    tokens = packs[0].shape[1]
    for place, out in enumerate(outs):
        out[1] = grad_keys[place * tokens : (place + 1) * tokens].astype(BF)
        out[2] = grad_values[place * tokens : (place + 1) * tokens].astype(BF)


def attention_backward(packs, grads, after):
    blocks = len(packs)
    _, tokens, width = packs[0].shape
    heads = width // HD
    pack_spec = pl.BlockSpec((3, tokens, HD), lambda h: (0, 0, h))
    row_spec = pl.BlockSpec((tokens, HD), lambda h: (0, h))
    return pl.pallas_call(
        functools.partial(backward_body, blocks),
        grid=(heads,),
        in_specs=[pack_spec] * blocks + [row_spec] * blocks + [pl.BlockSpec(memory_space=pl.ANY)],
        out_specs=[pack_spec] * blocks,
        out_shape=[jax.ShapeDtypeStruct((3, tokens, width), BF)] * blocks,
        cost_estimate=pl.CostEstimate(
            flops=10 * heads * (blocks * tokens) ** 2 * HD,
            bytes_accessed=14 * blocks * tokens * width,
            transcendentals=heads * (blocks * tokens) ** 2,
        ),
        name="attend_back",
    )(*packs, *grads, after)


class Links:
    def __init__(self):
        self.dp, self.seq = lax.axis_size("dp"), lax.axis_size("seq")
        self.pair = 2 if self.seq % 2 == 0 else 1
        self.chips = self.seq // self.pair
        self.d, self.s = lax.axis_index("dp"), lax.axis_index("seq")
        half = self.dp // 2
        if self.dp % 2:
            self.order = list(range(self.dp))
        else:
            self.order = [2 * i for i in range(half)] + [2 * i + 1 for i in reversed(range(half))]

    def table(self):
        lines = []
        for d in range(self.dp):
            place = self.order.index(d)
            behind = [self.order[(place - r) % self.dp] for r in range(self.dp)]
            ahead = [self.order[(place + r) % self.dp] for r in range(self.dp)]
            for s in range(self.seq):
                peers = [self.peer(s, k) for k in range(self.seq)]
                lines.append([s % self.pair] + peers + behind + ahead)
        return lines

    def permute(self, array, dp_to, seq_to):
        pairs = []
        for d in range(self.dp):
            for s in range(self.seq):
                pairs.append((d * self.seq + s, dp_to(d) * self.seq + seq_to(s)))
        return lax.ppermute(array, ("dp", "seq"), pairs)

    def ring(self, array, step):
        place = {d: i for i, d in enumerate(self.order)}
        return self.permute(array, lambda d: self.order[(place[d] + step) % self.dp], lambda s: s)

    def peer(self, s, k):
        chip, core = s // self.pair, s % self.pair
        return (chip + k // self.pair) % self.chips * self.pair + (core + k % self.pair) % self.pair

    def source(self, s, k):
        chip, core = s // self.pair, s % self.pair
        return (chip - k // self.pair) % self.chips * self.pair + (core - k % self.pair) % self.pair

    def out(self, array, k):
        return self.permute(array, lambda d: d, lambda s: self.peer(s, k))

    def back(self, array, k):
        return self.permute(array, lambda d: d, lambda s: self.source(s, k))

    def swap(self, array):
        return self.out(array, 1) if self.pair == 2 else array


def gather_ring(links, piece, forward):
    found = {0: piece}
    ahead, behind = piece, piece
    for step in range(1, max(forward, links.dp - 1 - forward) + 1):
        if step <= forward:
            ahead = links.ring(ahead, 1)
            found[step] = ahead
        if step <= links.dp - 1 - forward:
            behind = links.ring(behind, -1)
            found[links.dp - step] = behind
    return [found[r] for r in range(links.dp)]


def plus(a, b):
    return (a.astype(F32) + b.astype(F32)).astype(BF)


def reduce_ring(links, blocks, forward):
    backward = links.dp - 1 - forward
    ahead = behind = None
    for step in range(max(forward, backward)):
        if step < forward:
            block = blocks[forward - step]
            ahead = block if ahead is None else plus(ahead, block)
            ahead = links.ring(ahead, 1)
        if step < backward:
            block = blocks[links.dp - (backward - step)]
            behind = block if behind is None else plus(behind, block)
            behind = links.ring(behind, -1)
    total = blocks[0].astype(F32)
    for part in (ahead, behind):
        if part is not None:
            total = total + part.astype(F32)
    return total


VMEM_SPEC = pl.BlockSpec(memory_space=pltpu.VMEM)
SMEM_SPEC = pl.BlockSpec(memory_space=pltpu.SMEM)
ANY_SPEC = pl.BlockSpec(memory_space=pl.ANY)


def at(start, size):
    return pl.ds(pl.multiple_of(start, HD), size)


def call(body, operands, specs, shapes, scratch=(), flops=0):
    moved = sum(a.size * a.dtype.itemsize for a in operands)
    moved += sum(math.prod(a.shape) * a.dtype.itemsize for a in shapes)
    return pl.pallas_call(
        body,
        in_specs=specs,
        out_specs=[VMEM_SPEC] * len(shapes),
        out_shape=shapes,
        scratch_shapes=list(scratch),
        cost_estimate=pl.CostEstimate(flops=flops + moved, bytes_accessed=moved, transcendentals=0),
        compiler_params=pltpu.CompilerParams(vmem_limit_bytes=58 * 1024 * 1024),
    )(*operands)


def cut_weights(core, lift, out, gate, pair):
    rows, units = lift.shape
    gate_rows, feat = gate.shape
    strips, part = rows // gate_rows, units // pair
    strip = feat // pair // strips
    z_part = out.shape[1] // pair

    def body(core_ref, lift_ref, out_ref, gate_ref, *outs):
        for j in range(pair):
            c = (core_ref[0] + j) % pair
            first, second = outs[2 * j], outs[2 * j + 1]
            first[:, :part] = lift_ref[:, at(c * part, part)]
            for q in range(strips):
                first[q * gate_rows : (q + 1) * gate_rows, part:] = gate_ref[
                    :, at((c * strips + q) * strip, strip)
                ]
            second[...] = out_ref[:, at(c * z_part, z_part)]

    shapes = [
        jax.ShapeDtypeStruct((rows, part + strip), BF),
        jax.ShapeDtypeStruct((out.shape[0], z_part), BF),
    ] * pair
    return call(body, (core, lift, out, gate), [SMEM_SPEC] + [VMEM_SPEC] * 3, shapes)


def pack_inputs(owners, queries, keys, values, encoder, target, width):
    tokens, z_width = encoder.shape
    n_seq = queries.shape[1] // width

    def body(owner_ref, q_ref, k_ref, v_ref, e_ref, t_ref, *outs):
        for k in range(n_seq):
            for i, ref in enumerate((q_ref, k_ref, v_ref)):
                outs[k][i] = ref[:, at(owner_ref[k] * width, width)]
        rows = outs[n_seq]
        rows[:, :z_width] = e_ref[...]
        line = lax.broadcasted_iota(jnp.int32, (tokens, tokens), 0)
        lane = lax.broadcasted_iota(jnp.int32, (tokens, tokens), 1)
        place = jnp.sum(
            jnp.where(line == lane, jnp.broadcast_to(t_ref[...], (tokens, tokens)), 0).astype(F32),
            axis=1,
            keepdims=True,
        )
        high = jnp.floor(place * (1.0 / 256.0))
        low = place - 256.0 * high
        side = lax.broadcasted_iota(jnp.int32, (tokens, HD), 1)
        rows[:, z_width:] = jnp.where(side == 0, high, jnp.where(side == 1, low, 0.0)).astype(BF)

    shapes = [jax.ShapeDtypeStruct((3, tokens, width), BF)] * n_seq
    shapes.append(jax.ShapeDtypeStruct((tokens, z_width + HD), BF))
    return call(
        body,
        (owners, queries, keys, values, encoder, target),
        [SMEM_SPEC] + [VMEM_SPEC] * 5,
        shapes,
    )


def align_features(first_token, rows, tokens, gain, bias):
    z_width = gain.shape[1]

    def body(token_ref, gain_ref, bias_ref, *refs):
        out = refs[-1]
        picked = None
        for ref in refs[:-1]:
            count = ref.shape[0]
            place = ref[:, z_width:].astype(F32)
            target = place[:, 0:1] * 256.0 + place[:, 1:2]
            here = lax.broadcasted_iota(jnp.int32, (count, tokens), 1) + token_ref[1] * tokens
            chosen = jnp.where(target == here.astype(F32), 1.0, 0.0).astype(BF)
            part = tn(chosen, ref[:, :z_width])
            picked = part if picked is None else picked + part
        centred = picked - jnp.mean(picked, axis=-1, keepdims=True)
        variance = jnp.mean(centred * centred, axis=-1, keepdims=True)
        out[...] = (
            centred * lax.rsqrt(variance + EPSILON) * gain_ref[...] + bias_ref[...]
        ).astype(BF)

    return call(
        body,
        (first_token, gain, bias, *rows),
        [SMEM_SPEC] + [VMEM_SPEC] * (2 + len(rows)),
        [jax.ShapeDtypeStruct((tokens, z_width), BF)],
        flops=2 * tokens * sum(r.shape[0] for r in rows) * z_width,
    )[0]


def project(index, spread, residual, aligned, mixed, firsts, seconds, sizes):
    n_dp, n_seq, pair, units, strips = sizes
    tokens, feat = residual.shape
    z_width = aligned.shape[1]
    width = feat // n_seq
    rows, first_cols = firsts[0][0].shape
    part, strip = units // pair, first_cols - units // pair
    out_rows, z_part = seconds[0][0].shape
    n_pieces = n_dp * pair

    def body(index_ref, spread_ref, residual_ref, aligned_ref, *refs):
        refs = list(refs)
        take = lambda n: [refs.pop(0) for _ in range(n)]
        mixed_refs, first_refs, second_refs = take(n_seq), take(n_pieces), take(n_pieces)
        sent, kept, grad_gating = take(3)
        grad_pieces = take(n_seq)
        lift, out, gate, gating, hidden, grad_hidden, sems = refs
        core = index_ref[0]

        copies = []
        for r in range(n_dp):
            d = index_ref[1 + n_seq + r]
            for j in range(pair):
                c = (core + j) % pair
                i = r * pair + j
                copies.append(
                    (
                        pltpu.make_async_copy(
                            first_refs[i].at[:, pl.ds(part, strip)],
                            gate.at[c, pl.ds(pl.multiple_of(d * rows, rows), rows), :],
                            sems.at[0, i],
                        ),
                        pltpu.make_async_copy(
                            first_refs[i].at[:, pl.ds(0, part)],
                            lift.at[pl.ds(pl.multiple_of(d * rows, rows), rows), at(c * part, part)],
                            sems.at[1, i],
                        ),
                        pltpu.make_async_copy(
                            second_refs[i],
                            out.at[
                                pl.ds(pl.multiple_of(d * out_rows, out_rows), out_rows),
                                at(c * z_part, z_part),
                            ],
                            sems.at[2, i],
                        ),
                    )
                )
        for kind in range(3):
            for copy in copies:
                copy[kind].start()
        for copy in copies:
            copy[0].wait()
        for c in range(pair):
            lines = nn(spread_ref[...], gate[c])
            for q in range(strips):
                start = (c * strips + q) * strip
                gating[:, start : start + strip] = lines[q : q + 1, :]
        for k in range(n_seq):
            here = at(index_ref[1 + k] * width, width)
            hidden[:, here] = (
                residual_ref[:, here].astype(F32) + gating[:, here] * mixed_refs[k][...].astype(F32)
            ).astype(BF)
        for copy in copies:
            copy[1].wait()
        lifted = nn(hidden[...], lift[...])
        sigmoid = 1.0 / (1.0 + jnp.exp(-lifted))
        activated = (lifted * sigmoid).astype(BF)
        slope = sigmoid * (1.0 + lifted * (1.0 - sigmoid))
        for copy in copies:
            copy[2].wait()
        predicted = nn(activated, out[...])
        target = aligned_ref[...].astype(F32)
        pred_norm = jnp.sqrt(jnp.sum(predicted * predicted, axis=1, keepdims=True) + EPSILON)
        target_norm = jnp.sqrt(jnp.sum(target * target, axis=1, keepdims=True) + EPSILON)
        cosine = jnp.sum(predicted * target, axis=1, keepdims=True) / (pred_norm * target_norm)
        scale = -1.0 * z_width / (pred_norm * target_norm)
        pull = z_width * cosine / (pred_norm * pred_norm)
        grad_pred = (scale * target + pull * predicted).astype(BF)
        grad_lifted = (nt(grad_pred, out[...]) * slope).astype(BF)
        sent[:, :feat] = hidden[...]
        sent[:, feat : feat + units] = activated
        grad_hidden[...] = nt(grad_lifted, lift[...])
        lift[:tokens, :units] = grad_lifted
        out[:tokens, :z_width] = grad_pred
        other = (core + pair - 1) % pair
        sent[:, feat + units : feat + units + part] = lift[:tokens, at(other * part, part)]
        sent[:, feat + units + part :] = out[:tokens, at(other * z_part, z_part)]
        kept[:, :part] = lift[:tokens, at(core * part, part)]
        kept[:, part:] = out[:tokens, at(core * z_part, z_part)]
        for k in range(n_seq):
            here = at(index_ref[1 + k] * width, width)
            grads = grad_hidden[:, here]
            grad_pieces[k][...] = (gating[:, here] * grads).astype(BF)
            grad_gating[:, here] = jnp.sum(
                grads * mixed_refs[k][...].astype(F32), axis=0, keepdims=True
            )

    shapes = [
        jax.ShapeDtypeStruct((tokens, feat + units + part + z_part), BF),
        jax.ShapeDtypeStruct((tokens, part + z_part), BF),
        jax.ShapeDtypeStruct((1, feat), F32),
    ] + [jax.ShapeDtypeStruct((tokens, width), BF)] * n_seq
    flat = lambda pieces: [p for both in pieces for p in both]
    return call(
        body,
        (index, spread, residual, aligned, *mixed, *flat(firsts), *flat(seconds)),
        [SMEM_SPEC] + [VMEM_SPEC] * (3 + n_seq) + [ANY_SPEC] * (2 * n_pieces),
        shapes,
        [
            pltpu.VMEM((n_dp * rows, units), BF),
            pltpu.VMEM((n_dp * out_rows, z_width), BF),
            pltpu.VMEM((pair, n_dp * rows, strip), BF),
            pltpu.VMEM((1, feat), F32),
            pltpu.VMEM((tokens, feat), BF),
            pltpu.VMEM((tokens, feat), F32),
            pltpu.SemaphoreType.DMA((3, n_pieces)),
        ],
        flops=6 * tokens * units * (feat + z_width),
    )


def out_blocks(index, sent, got, kept, sizes, z_part, out_rows):
    n_dp, n_seq, pair, units, _ = sizes
    tokens, cols = sent.shape
    act = cols - units - units // pair - z_part
    halves = [sent] if got is None else [sent, got]

    def body(index_ref, kept_ref, *refs):
        sources, outs = refs[: len(halves)], refs[len(halves) :]
        grads = [kept_ref[:, units // pair :]]
        if got is not None:
            grads.append(sources[1][:, cols - z_part :])
        grads = jnp.concatenate(grads, axis=0)
        for r in range(n_dp):
            here = at(act + index_ref[1 + n_seq + n_dp + r] * out_rows, out_rows)
            left = jnp.concatenate([s[:, here] for s in sources], axis=0)
            outs[r][...] = tn(left, grads).astype(BF)

    return call(
        body,
        (index, kept, *halves),
        [SMEM_SPEC] + [VMEM_SPEC] * (1 + len(halves)),
        [jax.ShapeDtypeStruct((out_rows, z_part), BF)] * n_dp,
        flops=4 * tokens * z_part * units,
    )


def lift_blocks(index, sent, got, kept, grad_gating, embedded, sizes, rows, strip):
    n_dp, n_seq, pair, units, strips = sizes
    tokens, feat = sent.shape[0], n_dp * rows
    part, gate_rows = units // pair, rows // strips
    halves = [sent] if got is None else [sent, got]
    sums = len(grad_gating)

    def body(index_ref, kept_ref, embedded_ref, *refs):
        gating_refs, sources, outs = refs[:sums], refs[sums : sums + len(halves)], refs[sums + len(halves) :]
        grads = [kept_ref[:, :part]]
        if got is not None:
            grads.append(sources[1][:, feat + units : feat + units + part])
        grads = jnp.concatenate(grads, axis=0)
        core = index_ref[0]
        for r in range(n_dp):
            d = index_ref[1 + n_seq + n_dp + r]
            here = at(d * rows, rows)
            left = jnp.concatenate([s[:, here] for s in sources], axis=0)
            outs[r][:, :part] = tn(left, grads).astype(BF)
            line = embedded_ref[pl.ds(pl.multiple_of(d * gate_rows, gate_rows), gate_rows), :]
            for q in range(strips):
                there = at((core * strips + q) * strip, strip)
                gate = sum(g[:, there] for g in gating_refs)
                outs[r][q * gate_rows : (q + 1) * gate_rows, part:] = (line * gate).astype(BF)

    return call(
        body,
        (index, kept, embedded, *grad_gating, *halves),
        [SMEM_SPEC] + [VMEM_SPEC] * (2 + sums + len(halves)),
        [jax.ShapeDtypeStruct((rows, part + strip), BF)] * n_dp,
        flops=4 * tokens * part * feat,
    )


def place_lift(core, shares, sizes):
    _, _, pair, units, strips = sizes
    rows, cols = shares[0].shape
    part, strip = units // pair, cols - units // pair
    gate_rows = rows // strips

    def body(core_ref, *refs):
        shares_refs, (gate, lift) = refs[:pair], refs[pair:]
        for j in range(pair):
            c = (core_ref[0] + j) % pair
            lift[:, at(c * part, part)] = shares_refs[j][:, :part].astype(F32)
            for q in range(strips):
                gate[:, at((c * strips + q) * strip, strip)] = shares_refs[j][
                    q * gate_rows : (q + 1) * gate_rows, part:
                ].astype(F32)

    return call(
        body,
        (core, *shares),
        [SMEM_SPEC] + [VMEM_SPEC] * pair,
        [
            jax.ShapeDtypeStruct((gate_rows, strip * strips * pair), F32),
            jax.ShapeDtypeStruct((rows, units), F32),
        ],
    )


def place_out(core, shares, pair):
    out_rows, z_part = shares[0].shape

    def body(core_ref, *refs):
        for j in range(pair):
            c = (core_ref[0] + j) % pair
            refs[pair][:, at(c * z_part, z_part)] = refs[j][...].astype(F32)

    return call(
        body,
        (core, *shares),
        [SMEM_SPEC] + [VMEM_SPEC] * pair,
        [jax.ShapeDtypeStruct((out_rows, z_part * pair), F32)],
    )[0]


def place_grads(owners, pieces):
    _, tokens, width = pieces[0].shape

    def body(owner_ref, *refs):
        sources, outs = refs[: len(pieces)], refs[len(pieces) :]
        for k, ref in enumerate(sources):
            for i in range(3):
                outs[i][:, at(owner_ref[k] * width, width)] = ref[i]

    return call(
        body,
        (owners, *pieces),
        [SMEM_SPEC] + [VMEM_SPEC] * len(pieces),
        [jax.ShapeDtypeStruct((tokens, width * len(pieces)), BF)] * 3,
    )


def step(
    queries,
    key_states,
    value_states,
    residual,
    enc_hidden,
    enc_gain,
    enc_bias,
    feature_target,
    timestep,
    gate_weight,
    lift_weight,
    out_weight,
):
    links = Links()
    n_dp, n_seq, pair = links.dp, links.seq, links.pair
    tokens, feat = queries.shape[1:]
    width = feat // n_seq
    rows, units = lift_weight.shape
    gate_rows = gate_weight.shape[0]
    temb, strips = gate_rows * n_dp, rows // gate_rows
    sizes = (n_dp, n_seq, pair, units, strips)
    order = sorted(range(1, n_seq), key=lambda k: (k < pair, k))
    index = lax.dynamic_index_in_dim(
        jnp.asarray(links.table(), jnp.int32), links.d * n_seq + links.s, 0, False
    )
    owner_index = index[1 : 1 + n_seq]

    halves = cut_weights(index, lift_weight, out_weight, gate_weight, pair)
    ahead = n_dp // 2
    first_parts = gather_ring(links, halves[0], ahead)
    second_parts = gather_ring(links, halves[1], n_dp - 1 - ahead)

    def with_other(parts, own):
        if pair == 1:
            return [[p] for p in parts]
        return [[parts[0], own]] + [[p, links.swap(p)] for p in parts[1:]]

    firsts = with_other(first_parts, halves[2 * pair - 2])
    seconds = with_other(second_parts, halves[2 * pair - 1])

    packed = pack_inputs(
        owner_index,
        queries[0],
        key_states[0],
        value_states[0],
        enc_hidden[0],
        feature_target,
        width,
    )
    packs = [packed[0]] + [None] * (n_seq - 1)
    for k in order:
        packs[k] = links.out(packed[k], k)
    clip_rows = [packed[n_seq]]
    clip_rows += [links.out(packed[n_seq], j * pair) for j in range(1, links.chips)]
    if pair == 2:
        clip_rows += [links.swap(r) for r in clip_rows]
    aligned = align_features(
        index,
        clip_rows,
        tokens,
        enc_gain[None],
        enc_bias[None],
    )

    embedded = embed_time(timestep, temb)
    spread = (
        embedded.reshape(n_dp, 1, 1, gate_rows) * jnp.eye(strips, dtype=BF)[None, :, :, None]
    )
    spread = spread.transpose(1, 0, 2, 3).reshape(strips, n_dp * rows)
    tall = jnp.broadcast_to(embedded.astype(F32).reshape(temb, 1), (temb, feat // pair // strips))

    attended = attention_forward(packs)
    mixed = [attended[0]] + [None] * (n_seq - 1)
    for k in order:
        mixed[k] = links.back(attended[k], k)

    sent, kept, grad_gating, *pieces = project(
        index, spread, residual[0], aligned, mixed, firsts, seconds, sizes
    )
    got, gatings = None, [grad_gating]
    if pair == 2:
        got = links.swap(sent)
        gatings.append(links.swap(grad_gating))
    grads = [pieces[0]] + [None] * (n_seq - 1)
    for k in order:
        grads[k] = links.out(pieces[k], k)

    part_out = out_blocks(
        index, sent, got, kept, sizes, halves[1].shape[1], halves[1].shape[0]
    )
    part_lift = lift_blocks(
        index, sent, got, kept, gatings, tall, sizes, rows, feat // pair // strips
    )
    share_second = reduce_ring(links, part_out, n_dp - 1 - ahead)
    share_first = reduce_ring(links, part_lift, ahead)

    def over_seq(share):
        mine = share.astype(BF)
        total = share
        for j in range(1, links.chips):
            total = total + links.out(mine, j * pair).astype(F32)
        mine = total.astype(BF)
        return [mine] if pair == 1 else [mine, links.swap(mine)]

    grad_gate, grad_lift = place_lift(index, over_seq(share_first), sizes)
    grad_out = place_out(index, over_seq(share_second), pair)

    back = attention_backward(packs, grads, part_lift[0])
    done = [back[0]] + [None] * (n_seq - 1)
    for k in order:
        done[k] = links.back(back[k], k)
    d_queries, d_keys, d_values = place_grads(owner_index, done)
    return (d_queries[None], d_keys[None], d_values[None], grad_gate, grad_lift, grad_out)


def solution(mesh):
    in_specs = (
        P("dp", "seq", None),
        P("dp", "seq", None),
        P("dp", "seq", None),
        P("dp", "seq", None),
        P("dp", "seq", None),
        P(),
        P(),
        P("dp", "seq"),
        P("dp"),
        P("dp", None),
        P("dp", None),
        P("dp", None),
    )
    out_specs = (
        P("dp", "seq", None),
        P("dp", "seq", None),
        P("dp", "seq", None),
        P("dp", None),
        P("dp", None),
        P("dp", None),
    )
    return jax.shard_map(step, mesh=mesh, in_specs=in_specs, out_specs=out_specs, check_vma=False)
```

profile of v0, /device:TPU:0, one launch (start us, length us, event | category | flops | bytes accessed | tf_op | source)
XLA Modules:
  0.0 195.3 jit_solution(5998837776380894472)
XLA Ops:
  1.9 2.2 %shard_map.174 = (bf16[256,640]{1,0:T(8,128)(2,1)}, bf16[128,768]{1,0:T(8,128)(2,1)}, bf16[256,640]{1,0:T(8,128)(2,1)}, bf16[128,768]{1,0:T(8,128)(2,1)}) custom-call(s32[21]{0:T(128)} %get-tuple-element.96.token_ref.core_ref.index_ref, bf16[256,1024]{1,0:T(8,128)(2,1)} %lift_ref.1, bf16[128,1536]{1,0:T(8,128)(2,1)} %out_ref.1, bf16[32,2048]{1,0:T(8,128)(2,1)} %gate_ref.1), custom_call_target="tpu_custom_call" | custom-call | flops 2097236 | bytes 2097236 | tf_op jit(solution)/shard_map/pallas_call | solution.py:214
  4.1 3.0 %collective-permute-start.29 = (bf16[128,768]{1,0:T(8,128)(2,1)}, bf16[128,768]{1,0:T(8,128)(2,1)}, u32[]{:S(2)}, u32[]{:S(2)}) collective-permute-start(bf16[128,768]{1,0:T(8,128)(2,1)} %get-tuple-element.62.refs_20_), channel_id=1, source_target_pairs={{0,4},{1,5},{2,6},{3,7},{4,12},{5,13},{6,14},{7,15},{8,0},{9,1},{1... | collective-permute-start | bytes 589832 | tf_op jit(solution)/shard_map/ppermute | solution.py:142
  7.8 2.8 %shard_map.172 = (bf16[3,128,512]{2,1,0:T(8,128)(2,1)}, bf16[3,128,512]{2,1,0:T(8,128)(2,1)}, bf16[3,128,512]{2,1,0:T(8,128)(2,1)}, bf16[3,128,512]{2,1,0:T(8,128)(2,1)}, bf16[128,1664]{1,0:T(8,128)(2,1)}) custom-call(s32[4]{0:T(128)} %slice_bitcast_fusion.owner_ref, bf16[128,2048]{1,0:T(8,128)(2,1)} %bitcast.15, bf16[128,2048]{1,0:T(8,128)(2,1)} %bitcast.16, ...), custom_call_target="tpu_custom_call" | custom-call | flops 3965456 | bytes 3965456 | tf_op jit(solution)/shard_map/pallas_call | solution.py:214
  14.7 6.2 %collective-permute-done.9.refs_6_ = bf16[256,640]{1,0:T(8,128)(2,1)S(1)} collective-permute-done((bf16[256,640]{1,0:T(8,128)(2,1)S(1)}, bf16[256,640]{1,0:T(8,128)(2,1)S(1)}, u32[]{:S(2)}, u32[]{:S(2)}) %collective-permute-start.9) | collective-permute-done | bytes 327712 | tf_op jit(solution)/shard_map/ppermute | solution.py:142
  26.9 6.0 %collective-permute-done.2.refs_3_ = bf16[3,128,512]{2,1,0:T(8,128)(2,1)S(1)} collective-permute-done((bf16[3,128,512]{2,1,0:T(8,128)(2,1)}, bf16[3,128,512]{2,1,0:T(8,128)(2,1)S(1)}, u32[]{:S(2)}, u32[]{:S(2)}) %collective-permute-start.2) | collective-permute-done | bytes 393248 | tf_op jit(solution)/shard_map/ppermute | solution.py:142
  33.7 7.9 %attend.1 = (bf16[128,512]{1,0:T(8,128)(2,1)}, bf16[128,512]{1,0:T(8,128)(2,1)}, bf16[128,512]{1,0:T(8,128)(2,1)}, bf16[128,512]{1,0:T(8,128)(2,1)}) custom-call(bf16[3,128,512]{2,1,0:T(8,128)(2,1)} %get-tuple-element.51.refs_0_, bf16[3,128,512]{2,1,0:T(8,128)(2,1)} %copy-done.26, bf16[3,128,512]{2,1,0:T(8,128)(2,1)} %copy-done.27, ...), custom_call_target="tpu_custom_call" | custom-call | flops 536870912 | bytes 2097152 | tf_op jit(solution)/shard_map/attend/pallas_call | solution.py:54
  53.0 3.2 %collective-permute-done.27.refs_26_ = bf16[128,768]{1,0:T(8,128)(2,1)} collective-permute-done((bf16[128,768]{1,0:T(8,128)(2,1)S(1)}, bf16[128,768]{1,0:T(8,128)(2,1)}, u32[]{:S(2)}, u32[]{:S(2)}) %collective-permute-start.27) | collective-permute-done | bytes 196640 | tf_op jit(solution)/shard_map/ppermute | solution.py:142
  59.7 2.3 %collective-permute-done.18.refs_16_ = bf16[256,640]{1,0:T(8,128)(2,1)S(1)} collective-permute-done((bf16[256,640]{1,0:T(8,128)(2,1)S(1)}, bf16[256,640]{1,0:T(8,128)(2,1)S(1)}, u32[]{:S(2)}, u32[]{:S(2)}) %collective-permute-start.18) | collective-permute-done | bytes 327712 | tf_op jit(solution)/shard_map/ppermute | solution.py:142
  63.8 2.6 %collective-permute-done.13.refs_10_ = bf16[256,640]{1,0:T(8,128)(2,1)} collective-permute-done((bf16[256,640]{1,0:T(8,128)(2,1)S(1)}, bf16[256,640]{1,0:T(8,128)(2,1)}, u32[]{:S(2)}, u32[]{:S(2)}) %collective-permute-start.13) | collective-permute-done | bytes 327712 | tf_op jit(solution)/shard_map/ppermute | solution.py:142
  72.6 2.8 %collective-permute-done.19.refs_14_ = bf16[256,640]{1,0:T(8,128)(2,1)} collective-permute-done((bf16[256,640]{1,0:T(8,128)(2,1)S(1)}, bf16[256,640]{1,0:T(8,128)(2,1)}, u32[]{:S(2)}, u32[]{:S(2)}) %collective-permute-start.19) | collective-permute-done | bytes 327712 | tf_op jit(solution)/shard_map/ppermute | solution.py:142
  76.5 3.2 %shard_map.173.aligned_ref = bf16[128,1536]{1,0:T(8,128)(2,1)} custom-call(s32[21]{0:T(128)} %get-tuple-element.96.token_ref.core_ref.index_ref, f32[1,1536]{1,0:T(1,128)} %broadcast_in_dim.23.gain_ref, f32[1,1536]{1,0:T(1,128)} %broadcast_in_dim.24.bias_ref, bf16[128,1664]{1,0:T(8,128)(2,1)} %get-tuple-element.55.refs_0_, bf16[128,1664]{1,0:T(8,128)(2,1)} %copy-done.6, ...), custom_call_target="tpu_custom_call" | custom-call | flops 203436112 | bytes 2109524 | tf_op jit(solution)/shard_map/pallas_call | solution.py:214
  80.9 9.7 %shard_map.175 = (bf16[128,4352]{1,0:T(8,128)(2,1)}, bf16[128,1280]{1,0:T(8,128)(2,1)}, f32[1,2048]{1,0:T(1,128)}, bf16[128,512]{1,0:T(8,128)(2,1)}, bf16[128,51...) custom-call(s32[21]{0:T(128)} %get-tuple-element.96.token_ref.core_ref.index_ref, ...), custom_call_target="tpu_custom_call" | custom-call | flops 2830409728 | bytes 11837524 | tf_op jit(solution)/shard_map/pallas_call | solution.py:214
  91.3 2.5 %collective-permute-done.41.refs_3_.refs_1_ = bf16[128,4352]{1,0:T(8,128)(2,1)S(1)} collective-permute-done((bf16[128,4352]{1,0:T(8,128)(2,1)}, bf16[128,4352]{1,0:T(8,128)(2,1)S(1)}, u32[]{:S(2)}, u32[]{:S(2)}) %collective-permute-start.41) | collective-permute-done | bytes 1114144 | tf_op jit(solution)/shard_map/ppermute | solution.py:142
  94.7 3.1 %shard_map.179 = (bf16[128,768]{1,0:T(8,128)(2,1)}, bf16[128,768]{1,0:T(8,128)(2,1)}, bf16[128,768]{1,0:T(8,128)(2,1)}, bf16[128,768]{1,0:T(8,128)(2,1)}, bf16[1...) custom-call(s32[21]{0:T(128)} %get-tuple-element.96.token_ref.core_ref.index, ...), custom_call_target="tpu_custom_call" | custom-call | flops 406782048 | bytes 4128852 | tf_op jit(solution)/shard_map/pallas_call | solution.py:214
  100.5 3.8 %shard_map.176 = (bf16[256,640]{1,0:T(8,128)(2,1)}, bf16[256,640]{1,0:T(8,128)(2,1)}, bf16[256,640]{1,0:T(8,128)(2,1)}, bf16[256,640]{1,0:T(8,128)(2,1)}, bf16[2...) custom-call(s32[21]{0:T(128)} %get-tuple-element.96.token_ref.core_ref.index, ...), custom_call_target="tpu_custom_call" | custom-call | flops 542195776 | bytes 5324884 | tf_op jit(solution)/shard_map/pallas_call | solution.py:214
  108.6 5.6 %collective-permute-done.45 = bf16[256,640]{1,0:T(8,128)(2,1)S(1)} collective-permute-done((bf16[256,640]{1,0:T(8,128)(2,1)}, bf16[256,640]{1,0:T(8,128)(2,1)S(1)}, u32[]{:S(2)}, u32[]{:S(2)}) %collective-permute-start.45) | collective-permute-done | bytes 327712 | tf_op jit(solution)/shard_map/ppermute | solution.py:142
  118.7 3.0 %collective-permute-done.49 = bf16[256,640]{1,0:T(8,128)(2,1)S(1)} collective-permute-done((bf16[256,640]{1,0:T(8,128)(2,1)}, bf16[256,640]{1,0:T(8,128)(2,1)S(1)}, u32[]{:S(2)}, u32[]{:S(2)}) %collective-permute-start.49) | collective-permute-done | bytes 327712 | tf_op jit(solution)/shard_map/ppermute | solution.py:142
  122.3 5.1 %collective-permute-done.46 = bf16[256,640]{1,0:T(8,128)(2,1)S(1)} collective-permute-done((bf16[256,640]{1,0:T(8,128)(2,1)S(1)}, bf16[256,640]{1,0:T(8,128)(2,1)S(1)}, u32[]{:S(2)}, u32[]{:S(2)}) %collective-permute-start.46) | collective-permute-done | bytes 327712 | tf_op jit(solution)/shard_map/ppermute | solution.py:142
  129.6 5.7 %collective-permute-done.50 = bf16[256,640]{1,0:T(8,128)(2,1)S(1)} collective-permute-done((bf16[256,640]{1,0:T(8,128)(2,1)S(1)}, bf16[256,640]{1,0:T(8,128)(2,1)S(1)}, u32[]{:S(2)}, u32[]{:S(2)}) %collective-permute-start.50) | collective-permute-done | bytes 327712 | tf_op jit(solution)/shard_map/ppermute | solution.py:142
  138.2 4.9 %collective-permute-done.59 = bf16[128,768]{1,0:T(8,128)(2,1)S(1)} collective-permute-done((bf16[128,768]{1,0:T(8,128)(2,1)S(1)}, bf16[128,768]{1,0:T(8,128)(2,1)S(1)}, u32[]{:S(2)}, u32[]{:S(2)}) %collective-permute-start.59) | collective-permute-done | bytes 196640 | tf_op jit(solution)/shard_map/ppermute | solution.py:142
  143.2 3.5 %collective-permute-done.51 = bf16[256,640]{1,0:T(8,128)(2,1)S(1)} collective-permute-done((bf16[256,640]{1,0:T(8,128)(2,1)S(1)}, bf16[256,640]{1,0:T(8,128)(2,1)S(1)}, u32[]{:S(2)}, u32[]{:S(2)}) %collective-permute-start.51) | collective-permute-done | bytes 327712 | tf_op jit(solution)/shard_map/ppermute | solution.py:142
  151.1 10.3 %attend_back.1 = (bf16[3,128,512]{2,1,0:T(8,128)(2,1)}, bf16[3,128,512]{2,1,0:T(8,128)(2,1)}, bf16[3,128,512]{2,1,0:T(8,128)(2,1)}, bf16[3,128,512]{2,1,0:T(8,128)(2,1)}) custom-call(bf16[3,128,512]{2,1,0:T(8,128)(2,1)} %get-tuple-element.51.refs_0_, bf16[3,128,512]{2,1,0:T(8,128)(2,1)} %copy-done.26, bf16[3,128,512]{2,1,0:T(8,128)(2,1)} %copy-done.27, ...), custom_call_target="tpu_custom_call" | custom-call | flops 1342177280 | bytes 3670016 | tf_op jit(solution)/shard_map/attend_back/pallas_call | solution.py:99
  164.4 21.4 %collective-permute-done.61 = bf16[128,768]{1,0:T(8,128)(2,1)S(1)} collective-permute-done((bf16[128,768]{1,0:T(8,128)(2,1)S(1)}, bf16[128,768]{1,0:T(8,128)(2,1)S(1)}, u32[]{:S(2)}, u32[]{:S(2)}) %collective-permute-start.61) | collective-permute-done | bytes 196640 | tf_op jit(solution)/shard_map/ppermute | solution.py:142
  187.0 2.6 %shard_map.177 = (bf16[128,2048]{1,0:T(8,128)(2,1)}, bf16[128,2048]{1,0:T(8,128)(2,1)}, bf16[128,2048]{1,0:T(8,128)(2,1)}) custom-call(s32[4]{0:T(128)} %slice_bitcast_fusion.owner_ref, bf16[3,128,512]{2,1,0:T(8,128)(2,1)} %get-tuple-element.72.refs_0_, bf16[3,128,512]{2,1,0:T(8,128)(2,1)} %copy-done.9, bf16[3,128,512]{2,1,0:T(8,128)(2,1)} %copy-done.10, ...), custom_call_target="tpu_custom_call" | custom-call | flops 3145744 | bytes 3145744 | tf_op jit(solution)/shard_map/pallas_call | solution.py:214
  (255 shorter events, 69.8 us)
Async XLA Ops:
  10.6 13.6 %collective-permute-start = (bf16[3,128,512]{2,1,0:T(8,128)(2,1)}, bf16[3,128,512]{2,1,0:T(8,128)(2,1)S(1)}, u32[]{:S(2)}, u32[]{:S(2)}) collective-permute-start(bf16[3,128,512]{2,1,0:T(8,128)(2,1)} %get-tuple-element.52), channel_id=1, source_target_pairs={{0,1},{1,0},{2,3},{3,2},{4,5},{5,4},{6,7},{7,6},{8,9},{9,8},{10,11... | collective-permute-start | bytes 1179656 | tf_op jit(solution)/shard_map/ppermute | solution.py:142
  12.7 12.2 %collective-permute-start.1 = (bf16[3,128,512]{2,1,0:T(8,128)(2,1)}, bf16[3,128,512]{2,1,0:T(8,128)(2,1)S(1)}, u32[]{:S(2)}, u32[]{:S(2)}) collective-permute-start(bf16[3,128,512]{2,1,0:T(8,128)(2,1)} %get-tuple-element.53), channel_id=1, source_target_pairs={{0,2},{1,3},{2,0},{3,1},{4,6},{5,7},{6,4},{7,5},{8,10},{9,11},{10,... | collective-permute-start | bytes 1179656 | tf_op jit(solution)/shard_map/ppermute | solution.py:142
  14.7 18.2 %collective-permute-start.2 = (bf16[3,128,512]{2,1,0:T(8,128)(2,1)}, bf16[3,128,512]{2,1,0:T(8,128)(2,1)S(1)}, u32[]{:S(2)}, u32[]{:S(2)}) collective-permute-start(bf16[3,128,512]{2,1,0:T(8,128)(2,1)} %get-tuple-element.54), channel_id=1, source_target_pairs={{0,3},{1,2},{2,1},{3,0},{4,7},{5,6},{6,5},{7,4},{8,11},{9,10},{10,... | collective-permute-start | bytes 1179656 | tf_op jit(solution)/shard_map/ppermute | solution.py:142
  20.9 24.6 %collective-permute-start.3 = (bf16[128,1664]{1,0:T(8,128)(2,1)}, bf16[128,1664]{1,0:T(8,128)(2,1)S(1)}, u32[]{:S(2)}, u32[]{:S(2)}) collective-permute-start(bf16[128,1664]{1,0:T(8,128)(2,1)} %get-tuple-element.55.refs_0_), channel_id=1, source_target_pairs={{0,2},{1,3},{2,0},{3,1},{4,6},{5,7},{6,4},{7,5},{8,10},{9,11},{10,... | collective-permute-start | bytes 1277960 | tf_op jit(solution)/shard_map/ppermute | solution.py:142
  24.2 21.7 %collective-permute-start.4 = (bf16[128,1664]{1,0:T(8,128)(2,1)}, bf16[128,1664]{1,0:T(8,128)(2,1)S(1)}, u32[]{:S(2)}, u32[]{:S(2)}) collective-permute-start(bf16[128,1664]{1,0:T(8,128)(2,1)} %get-tuple-element.55.refs_0_), channel_id=1, source_target_pairs={{0,1},{1,0},{2,3},{3,2},{4,5},{5,4},{6,7},{7,6},{8,9},{9,8},{10,11... | collective-permute-start | bytes 1277960 | tf_op jit(solution)/shard_map/ppermute | solution.py:142
  24.9 16.7 %collective-permute-start.25 = (bf16[128,768]{1,0:T(8,128)(2,1)}, bf16[128,768]{1,0:T(8,128)(2,1)S(1)}, u32[]{:S(2)}, u32[]{:S(2)}) collective-permute-start(bf16[128,768]{1,0:T(8,128)(2,1)} %collective-permute-done.23.refs_22_), channel_id=1, source_target_pairs={{0,8},{1,9},{2,10},{3,11},{4,0},{5,1},{6,2},{7,3},{8,16},{9,17},{1... | collective-permute-start | bytes 589832 | tf_op jit(solution)/shard_map/ppermute | solution.py:142
  33.2 10.8 %collective-permute-start.36 = (bf16[128,768]{1,0:T(8,128)(2,1)}, bf16[128,768]{1,0:T(8,128)(2,1)}, u32[]{:S(2)}, u32[]{:S(2)}) collective-permute-start(bf16[128,768]{1,0:T(8,128)(2,1)} %collective-permute-done.29.refs_34_), channel_id=1, source_target_pairs={{0,1},{1,0},{2,3},{3,2},{4,5},{5,4},{6,7},{7,6},{8,9},{9,8},{10,11... | collective-permute-start | bytes 589832 | tf_op jit(solution)/shard_map/ppermute | solution.py:142
  42.0 14.2 %collective-permute-start.11 = (bf16[256,640]{1,0:T(8,128)(2,1)S(1)}, bf16[256,640]{1,0:T(8,128)(2,1)S(1)}, u32[]{:S(2)}, u32[]{:S(2)}) collective-permute-start(bf16[256,640]{1,0:T(8,128)(2,1)S(1)} %collective-permute-done.9.refs_6_), channel_id=1, source_target_pairs={{0,8},{1,9},{2,10},{3,11},{4,0},{5,1},{6,2},{7,3},{8,16},{9,17},{1... | collective-permute-start | bytes 983048 | tf_op jit(solution)/shard_map/ppermute | solution.py:142
  59.5 12.6 %collective-permute-start.5 = (bf16[128,1664]{1,0:T(8,128)(2,1)S(1)}, bf16[128,1664]{1,0:T(8,128)(2,1)S(1)}, u32[]{:S(2)}, u32[]{:S(2)}) collective-permute-start(bf16[128,1664]{1,0:T(8,128)(2,1)S(1)} %collective-permute-done.3.refs_1_), channel_id=1, source_target_pairs={{0,1},{1,0},{2,3},{3,2},{4,5},{5,4},{6,7},{7,6},{8,9},{9,8},{10,11... | collective-permute-start | bytes 1277960 | tf_op jit(solution)/shard_map/ppermute | solution.py:142
  62.2 13.1 %collective-permute-start.19 = (bf16[256,640]{1,0:T(8,128)(2,1)S(1)}, bf16[256,640]{1,0:T(8,128)(2,1)}, u32[]{:S(2)}, u32[]{:S(2)}) collective-permute-start(bf16[256,640]{1,0:T(8,128)(2,1)S(1)} %collective-permute-done.18.refs_16_), channel_id=1, source_target_pairs={{0,4},{1,5},{2,6},{3,7},{4,12},{5,13},{6,14},{7,15},{8,0},{9,1},{1... | collective-permute-start | bytes 983048 | tf_op jit(solution)/shard_map/ppermute | solution.py:142
  106.0 42.9 %collective-permute-start.37 = (bf16[128,512]{1,0:T(8,128)(2,1)S(1)}, bf16[128,512]{1,0:T(8,128)(2,1)S(1)}, u32[]{:S(2)}, u32[]{:S(2)}) collective-permute-start(bf16[128,512]{1,0:T(8,128)(2,1)S(1)} %copy-done.50), channel_id=1, source_target_pairs={{0,1},{1,0},{2,3},{3,2},{4,5},{5,4},{6,7},{7,6},{8,9},{9,8},{10,11... | collective-permute-start | bytes 393224 | tf_op jit(solution)/shard_map/ppermute | solution.py:142
  106.0 44.4 %collective-permute-start.38 = (bf16[128,512]{1,0:T(8,128)(2,1)S(1)}, bf16[128,512]{1,0:T(8,128)(2,1)S(1)}, u32[]{:S(2)}, u32[]{:S(2)}) collective-permute-start(bf16[128,512]{1,0:T(8,128)(2,1)S(1)} %copy-done.49), channel_id=1, source_target_pairs={{0,2},{1,3},{2,0},{3,1},{4,6},{5,7},{6,4},{7,5},{8,10},{9,11},{10,... | collective-permute-start | bytes 393224 | tf_op jit(solution)/shard_map/ppermute | solution.py:142
  108.2 13.5 %collective-permute-start.49 = (bf16[256,640]{1,0:T(8,128)(2,1)}, bf16[256,640]{1,0:T(8,128)(2,1)S(1)}, u32[]{:S(2)}, u32[]{:S(2)}) collective-permute-start(bf16[256,640]{1,0:T(8,128)(2,1)} %get-tuple-element.83), channel_id=1, source_target_pairs={{0,4},{1,5},{2,6},{3,7},{4,12},{5,13},{6,14},{7,15},{8,0},{9,1},{1... | collective-permute-start | bytes 983048 | tf_op jit(solution)/shard_map/ppermute | solution.py:142
  114.3 23.3 %collective-permute-start.55 = (bf16[128,768]{1,0:T(8,128)(2,1)S(1)}, bf16[128,768]{1,0:T(8,128)(2,1)S(1)}, u32[]{:S(2)}, u32[]{:S(2)}) collective-permute-start(bf16[128,768]{1,0:T(8,128)(2,1)S(1)} %add_convert_fusion.11), channel_id=1, source_target_pairs={{0,8},{1,9},{2,10},{3,11},{4,0},{5,1},{6,2},{7,3},{8,16},{9,17},{1... | collective-permute-start | bytes 589832 | tf_op jit(solution)/shard_map/ppermute | solution.py:142
  135.9 10.8 %collective-permute-start.51 = (bf16[256,640]{1,0:T(8,128)(2,1)S(1)}, bf16[256,640]{1,0:T(8,128)(2,1)S(1)}, u32[]{:S(2)}, u32[]{:S(2)}) collective-permute-start(bf16[256,640]{1,0:T(8,128)(2,1)S(1)} %add_convert_fusion.1), channel_id=1, source_target_pairs={{0,4},{1,5},{2,6},{3,7},{4,12},{5,13},{6,14},{7,15},{8,0},{9,1},{1... | collective-permute-start | bytes 983048 | tf_op jit(solution)/shard_map/ppermute | solution.py:142
  137.6 10.7 %collective-permute-start.48 = (bf16[256,640]{1,0:T(8,128)(2,1)S(1)}, bf16[256,640]{1,0:T(8,128)(2,1)S(1)}, u32[]{:S(2)}, u32[]{:S(2)}) collective-permute-start(bf16[256,640]{1,0:T(8,128)(2,1)S(1)} %add_convert_fusion.3), channel_id=1, source_target_pairs={{0,8},{1,9},{2,10},{3,11},{4,0},{5,1},{6,2},{7,3},{8,16},{9,17},{1... | collective-permute-start | bytes 983048 | tf_op jit(solution)/shard_map/ppermute | solution.py:142
  146.7 15.4 %collective-permute-start.56 = (bf16[128,768]{1,0:T(8,128)(2,1)S(1)}, bf16[128,768]{1,0:T(8,128)(2,1)S(1)}, u32[]{:S(2)}, u32[]{:S(2)}) collective-permute-start(bf16[128,768]{1,0:T(8,128)(2,1)S(1)} %add_convert_fusion.10), channel_id=1, source_target_pairs={{0,8},{1,9},{2,10},{3,11},{4,0},{5,1},{6,2},{7,3},{8,16},{9,17},{1... | collective-permute-start | bytes 589832 | tf_op jit(solution)/shard_map/ppermute | solution.py:142
  148.3 15.0 %collective-permute-start.60 = (bf16[128,768]{1,0:T(8,128)(2,1)S(1)}, bf16[128,768]{1,0:T(8,128)(2,1)S(1)}, u32[]{:S(2)}, u32[]{:S(2)}) collective-permute-start(bf16[128,768]{1,0:T(8,128)(2,1)S(1)} %add_convert_fusion.7), channel_id=1, source_target_pairs={{0,4},{1,5},{2,6},{3,7},{4,12},{5,13},{6,14},{7,15},{8,0},{9,1},{1... | collective-permute-start | bytes 589832 | tf_op jit(solution)/shard_map/ppermute | solution.py:142
  148.9 15.2 %collective-permute-start.52 = (bf16[256,640]{1,0:T(8,128)(2,1)S(1)}, bf16[256,640]{1,0:T(8,128)(2,1)S(1)}, u32[]{:S(2)}, u32[]{:S(2)}) collective-permute-start(bf16[256,640]{1,0:T(8,128)(2,1)S(1)} %fusion), channel_id=1, source_target_pairs={{0,2},{1,3},{2,0},{3,1},{4,6},{5,7},{6,4},{7,5},{8,10},{9,11},{10,... | collective-permute-start | bytes 983048 | tf_op jit(solution)/shard_map/ppermute | solution.py:142
  161.4 24.6 %collective-permute-start.42 = (bf16[3,128,512]{2,1,0:T(8,128)(2,1)}, bf16[3,128,512]{2,1,0:T(8,128)(2,1)S(1)}, u32[]{:S(2)}, u32[]{:S(2)}) collective-permute-start(bf16[3,128,512]{2,1,0:T(8,128)(2,1)} %get-tuple-element.73), channel_id=1, source_target_pairs={{0,1},{1,0},{2,3},{3,2},{4,5},{5,4},{6,7},{7,6},{8,9},{9,8},{10,11... | collective-permute-start | bytes 1179656 | tf_op jit(solution)/shard_map/ppermute | solution.py:142
  161.4 24.6 %collective-permute-start.43 = (bf16[3,128,512]{2,1,0:T(8,128)(2,1)}, bf16[3,128,512]{2,1,0:T(8,128)(2,1)S(1)}, u32[]{:S(2)}, u32[]{:S(2)}) collective-permute-start(bf16[3,128,512]{2,1,0:T(8,128)(2,1)} %get-tuple-element.74), channel_id=1, source_target_pairs={{0,2},{1,3},{2,0},{3,1},{4,6},{5,7},{6,4},{7,5},{8,10},{9,11},{10,... | collective-permute-start | bytes 1179656 | tf_op jit(solution)/shard_map/ppermute | solution.py:142
  162.1 23.9 %collective-permute-start.44 = (bf16[3,128,512]{2,1,0:T(8,128)(2,1)}, bf16[3,128,512]{2,1,0:T(8,128)(2,1)S(1)}, u32[]{:S(2)}, u32[]{:S(2)}) collective-permute-start(bf16[3,128,512]{2,1,0:T(8,128)(2,1)} %get-tuple-element.75), channel_id=1, source_target_pairs={{0,3},{1,2},{2,1},{3,0},{4,7},{5,6},{6,5},{7,4},{8,11},{9,10},{10,... | collective-permute-start | bytes 1179656 | tf_op jit(solution)/shard_map/ppermute | solution.py:142
  163.4 22.4 %collective-permute-start.61 = (bf16[128,768]{1,0:T(8,128)(2,1)S(1)}, bf16[128,768]{1,0:T(8,128)(2,1)S(1)}, u32[]{:S(2)}, u32[]{:S(2)}) collective-permute-start(bf16[128,768]{1,0:T(8,128)(2,1)S(1)} %fusion.1), channel_id=1, source_target_pairs={{0,2},{1,3},{2,0},{3,1},{4,6},{5,7},{6,4},{7,5},{8,10},{9,11},{10,... | collective-permute-start | bytes 589832 | tf_op jit(solution)/shard_map/ppermute | solution.py:142
  164.2 28.1 %collective-permute-start.53 = (bf16[256,640]{1,0:T(8,128)(2,1)S(1)}, bf16[256,640]{1,0:T(8,128)(2,1)S(1)}, u32[]{:S(2)}, u32[]{:S(2)}) collective-permute-start(bf16[256,640]{1,0:T(8,128)(2,1)S(1)} %add_convert_fusion.refs_0_), channel_id=1, source_target_pairs={{0,1},{1,0},{2,3},{3,2},{4,5},{5,4},{6,7},{7,6},{8,9},{9,8},{10,11... | collective-permute-start | bytes 983048 | tf_op jit(solution)/shard_map/ppermute | solution.py:142
  (95 other events, 999.0 us)
where the time goes:
time: 196 us; the launch traced here: 195 us
  waiting for transfers between devices  81.6 us (42%)
  Pallas kernels  49.9 us (25%)
  starting transfers between devices  48 us (24%)
  local copies, waits for them, and re-layouts  11 us (6%)
  other arithmetic  2.88 us (1%)
    ppermute x63, waiting for transfers between devices, permute(): return lax.ppermute(array, ('dp', 'seq'), pairs)  81.6 us
    ppermute x63, starting transfers between devices, permute(): return lax.ppermute(array, ('dp', 'seq'), pairs)  48 us
    pallas_call x9, Pallas kernels, call(): pl.pallas_call(body, in_specs=specs, out_specs=[VMEM_SPEC] * len(shapes),...  31.7 us
    pallas_call x1, Pallas kernels, attention_backward(): pl.pallas_call(functools.partial(backward_body, blocks), grid=(heads,), i...  10.3 us
    pallas_call x1, Pallas kernels, attention_forward(): pl.pallas_call(functools.partial(forward_body, blocks), grid=(heads,), in...  7.93 us
    unnamed x112, local copies, waits for them, and re-layouts  6.75 us
  transfers between devices with their start and end apart: 63, of which 21 were waited for; matrix products, arithmetic and copies ran while one was open for 3% of the time, Pallas kernels for 18%

commit v1 on v0

--- a/solution.py
+++ b/solution.py
@@ -36,15 +36,37 @@
     return lax.dot_general(a, b, (((0,), (0,)), ((), ())), preferred_element_type=F32)
 
 
+def group_of(tokens, blocks):
+    count = max(1, 256 // tokens)
+    return count if blocks % count == 0 else 1
+
+
+def joined(parts):
+    return parts[0] if len(parts) == 1 else jnp.concatenate(parts, axis=0)
+
+
+SCALE = HD ** (-0.5)
+
+
+def soft_columns(keys, query):
+    scores = nt(keys, query)
+    shifted = jnp.exp2(
+        (scores - jnp.max(scores, axis=0, keepdims=True)) * (SCALE * math.log2(math.e))
+    )
+    return shifted, 1.0 / jnp.sum(shifted, axis=0, keepdims=True)
+
+
 def forward_body(blocks, *refs):
     packs, outs = refs[:blocks], refs[blocks:]
-    keys = jnp.concatenate([p[1] for p in packs], axis=0)
-    values = jnp.concatenate([p[2] for p in packs], axis=0)
-    for pack, out in zip(packs, outs):
-        scores = nt(pack[0], keys) * HD ** (-0.5)
-        shifted = jnp.exp(scores - jnp.max(scores, axis=-1, keepdims=True))
-        chances = shifted / jnp.sum(shifted, axis=-1, keepdims=True)
-        out[...] = nn(chances.astype(BF), values).astype(BF)
+    tokens = packs[0].shape[1]
+    step = group_of(tokens, blocks)
+    keys = joined([p[1] for p in packs])
+    values = joined([p[2] for p in packs])
+    for first in range(0, blocks, step):
+        shifted, inverse = soft_columns(keys, joined([p[0] for p in packs[first : first + step]]))
+        mixed = (tn(values, shifted.astype(BF)) * inverse).T.astype(BF)
+        for i in range(step):
+            outs[first + i][...] = mixed[i * tokens : (i + 1) * tokens]
 
 
 def attention_forward(packs):
@@ -68,25 +90,28 @@
 
 def backward_body(blocks, *refs):
     packs, grads, outs = refs[:blocks], refs[blocks : 2 * blocks], refs[2 * blocks + 1 :]
-    keys = jnp.concatenate([p[1] for p in packs], axis=0)
-    values = jnp.concatenate([p[2] for p in packs], axis=0)
+    tokens = packs[0].shape[1]
+    step = group_of(tokens, blocks)
+    keys = joined([p[1] for p in packs])
+    values = joined([p[2] for p in packs])
     grad_keys = grad_values = None
-    for pack, grad, out in zip(packs, grads, outs):
-        query, grad_rows = pack[0], grad[...]
-        scores = nt(keys, query) * HD ** (-0.5)
-        shifted = jnp.exp(scores - jnp.max(scores, axis=0, keepdims=True))
-        chances = shifted / jnp.sum(shifted, axis=0, keepdims=True)
+    for first in range(0, blocks, step):
+        query = joined([p[0] for p in packs[first : first + step]])
+        grad_rows = joined([g[...] for g in grads[first : first + step]])
+        shifted, inverse = soft_columns(keys, query)
+        chances = shifted * inverse
         grad_chances = nt(values, grad_rows)
         add_values = nn(chances.astype(BF), grad_rows)
         inner = jnp.sum(grad_chances * chances, axis=0, keepdims=True)
-        grad_scores = (chances * (grad_chances - inner) * HD ** (-0.5)).astype(BF)
-        out[0] = tn(grad_scores, keys).astype(BF)
+        grad_scores = (chances * (grad_chances - inner)).astype(BF)
+        grad_query = (tn(keys, grad_scores) * SCALE).T.astype(BF)
+        for i in range(step):
+            outs[first + i][0] = grad_query[i * tokens : (i + 1) * tokens]
         add_keys = nn(grad_scores, query)
         grad_keys = add_keys if grad_keys is None else grad_keys + add_keys
         grad_values = add_values if grad_values is None else grad_values + add_values
-    tokens = packs[0].shape[1]
     for place, out in enumerate(outs):
-        out[1] = grad_keys[place * tokens : (place + 1) * tokens].astype(BF)
+        out[1] = (grad_keys[place * tokens : (place + 1) * tokens] * SCALE).astype(BF)
         out[2] = grad_values[place * tokens : (place + 1) * tokens].astype(BF)
 
 

time: 196 us -> 191 us (0.974)
  Pallas kernels: 49.9 us -> 45.1 us
    pallas_call x1, Pallas kernels: 10.3 us -> 7.4 us  [attention_backward(): pl.pallas_call(functools.partial(backward_body, blocks), grid=(heads,), i...]
  transfers between devices with their start and end apart: 63 -> 63, of which waited for: 21 -> 21; matrix products, arithmetic and copies ran while one was open for 3% -> 3% of each run, Pallas kernels for 18% -> 16%
where the time goes in v1:
time: 191 us; the launch traced here: 190 us
  waiting for transfers between devices  81.3 us (43%)
  starting transfers between devices  48.3 us (25%)
  Pallas kernels  45.1 us (24%)
  local copies, waits for them, and re-layouts  11 us (6%)
  other arithmetic  2.88 us (2%)
    ppermute x63, waiting for transfers between devices, permute(): return lax.ppermute(array, ('dp', 'seq'), pairs)  81.3 us
    ppermute x63, starting transfers between devices, permute(): return lax.ppermute(array, ('dp', 'seq'), pairs)  48.3 us
    pallas_call x9, Pallas kernels, call(): pl.pallas_call(body, in_specs=specs, out_specs=[VMEM_SPEC] * len(shapes),...  31.7 us
    pallas_call x1, Pallas kernels, attention_backward(): pl.pallas_call(functools.partial(backward_body, blocks), grid=(heads,), i...  7.4 us
    unnamed x112, local copies, waits for them, and re-layouts  6.75 us
    pallas_call x1, Pallas kernels, attention_forward(): pl.pallas_call(functools.partial(forward_body, blocks), grid=(heads,), in...  6 us
  transfers between devices with their start and end apart: 63, of which 21 were waited for; matrix products, arithmetic and copies ran while one was open for 3% of the time, Pallas kernels for 16%

profile of v1, /device:TPU:0, one launch (start us, length us, event | category | flops | bytes accessed | tf_op | source)
XLA Modules:
  0.0 190.4 jit_solution(14744661588291738089)
XLA Ops:
  1.9 2.2 %shard_map.174 = (bf16[256,640]{1,0:T(8,128)(2,1)}, bf16[128,768]{1,0:T(8,128)(2,1)}, bf16[256,640]{1,0:T(8,128)(2,1)}, bf16[128,768]{1,0:T(8,128)(2,1)}) custom-call(s32[21]{0:T(128)} %get-tuple-element.96.token_ref.core_ref.index_ref, bf16[256,1024]{1,0:T(8,128)(2,1)} %lift_ref.1, bf16[128,1536]{1,0:T(8,128)(2,1)} %out_ref.1, bf16[32,2048]{1,0:T(8,128)(2,1)} %gate_ref.1), custom_call_target="tpu_custom_call" | custom-call | flops 2097236 | bytes 2097236 | tf_op jit(solution)/shard_map/pallas_call | solution.py:239
  4.1 3.0 %collective-permute-start.29 = (bf16[128,768]{1,0:T(8,128)(2,1)}, bf16[128,768]{1,0:T(8,128)(2,1)}, u32[]{:S(2)}, u32[]{:S(2)}) collective-permute-start(bf16[128,768]{1,0:T(8,128)(2,1)} %get-tuple-element.62.refs_20_), channel_id=1, source_target_pairs={{0,4},{1,5},{2,6},{3,7},{4,12},{5,13},{6,14},{7,15},{8,0},{9,1},{1... | collective-permute-start | bytes 589832 | tf_op jit(solution)/shard_map/ppermute | solution.py:167
  7.8 2.8 %shard_map.172 = (bf16[3,128,512]{2,1,0:T(8,128)(2,1)}, bf16[3,128,512]{2,1,0:T(8,128)(2,1)}, bf16[3,128,512]{2,1,0:T(8,128)(2,1)}, bf16[3,128,512]{2,1,0:T(8,128)(2,1)}, bf16[128,1664]{1,0:T(8,128)(2,1)}) custom-call(s32[4]{0:T(128)} %slice_bitcast_fusion.owner_ref, bf16[128,2048]{1,0:T(8,128)(2,1)} %bitcast.15, bf16[128,2048]{1,0:T(8,128)(2,1)} %bitcast.16, ...), custom_call_target="tpu_custom_call" | custom-call | flops 3965456 | bytes 3965456 | tf_op jit(solution)/shard_map/pallas_call | solution.py:239
  14.7 6.2 %collective-permute-done.9.refs_6_ = bf16[256,640]{1,0:T(8,128)(2,1)S(1)} collective-permute-done((bf16[256,640]{1,0:T(8,128)(2,1)S(1)}, bf16[256,640]{1,0:T(8,128)(2,1)S(1)}, u32[]{:S(2)}, u32[]{:S(2)}) %collective-permute-start.9) | collective-permute-done | bytes 327712 | tf_op jit(solution)/shard_map/ppermute | solution.py:167
  26.9 6.0 %collective-permute-done.2.refs_3_ = bf16[3,128,512]{2,1,0:T(8,128)(2,1)S(1)} collective-permute-done((bf16[3,128,512]{2,1,0:T(8,128)(2,1)}, bf16[3,128,512]{2,1,0:T(8,128)(2,1)S(1)}, u32[]{:S(2)}, u32[]{:S(2)}) %collective-permute-start.2) | collective-permute-done | bytes 393248 | tf_op jit(solution)/shard_map/ppermute | solution.py:167
  33.7 6.0 %attend.1 = (bf16[128,512]{1,0:T(8,128)(2,1)}, bf16[128,512]{1,0:T(8,128)(2,1)}, bf16[128,512]{1,0:T(8,128)(2,1)}, bf16[128,512]{1,0:T(8,128)(2,1)}) custom-call(bf16[3,128,512]{2,1,0:T(8,128)(2,1)} %get-tuple-element.51.refs_0_, bf16[3,128,512]{2,1,0:T(8,128)(2,1)} %copy-done.26, bf16[3,128,512]{2,1,0:T(8,128)(2,1)} %copy-done.27, ...), custom_call_target="tpu_custom_call" | custom-call | flops 536870912 | bytes 2097152 | tf_op jit(solution)/shard_map/attend/pallas_call | solution.py:76
  51.1 3.1 %collective-permute-done.27.refs_26_ = bf16[128,768]{1,0:T(8,128)(2,1)} collective-permute-done((bf16[128,768]{1,0:T(8,128)(2,1)S(1)}, bf16[128,768]{1,0:T(8,128)(2,1)}, u32[]{:S(2)}, u32[]{:S(2)}) %collective-permute-start.27) | collective-permute-done | bytes 196640 | tf_op jit(solution)/shard_map/ppermute | solution.py:167
  57.7 2.3 %collective-permute-done.18.refs_16_ = bf16[256,640]{1,0:T(8,128)(2,1)S(1)} collective-permute-done((bf16[256,640]{1,0:T(8,128)(2,1)S(1)}, bf16[256,640]{1,0:T(8,128)(2,1)S(1)}, u32[]{:S(2)}, u32[]{:S(2)}) %collective-permute-start.18) | collective-permute-done | bytes 327712 | tf_op jit(solution)/shard_map/ppermute | solution.py:167
  61.9 2.5 %collective-permute-done.13.refs_10_ = bf16[256,640]{1,0:T(8,128)(2,1)} collective-permute-done((bf16[256,640]{1,0:T(8,128)(2,1)S(1)}, bf16[256,640]{1,0:T(8,128)(2,1)}, u32[]{:S(2)}, u32[]{:S(2)}) %collective-permute-start.13) | collective-permute-done | bytes 327712 | tf_op jit(solution)/shard_map/ppermute | solution.py:167
  70.6 2.8 %collective-permute-done.19.refs_14_ = bf16[256,640]{1,0:T(8,128)(2,1)} collective-permute-done((bf16[256,640]{1,0:T(8,128)(2,1)S(1)}, bf16[256,640]{1,0:T(8,128)(2,1)}, u32[]{:S(2)}, u32[]{:S(2)}) %collective-permute-start.19) | collective-permute-done | bytes 327712 | tf_op jit(solution)/shard_map/ppermute | solution.py:167
  74.6 3.2 %shard_map.173.aligned_ref = bf16[128,1536]{1,0:T(8,128)(2,1)} custom-call(s32[21]{0:T(128)} %get-tuple-element.96.token_ref.core_ref.index_ref, f32[1,1536]{1,0:T(1,128)} %broadcast_in_dim.23.gain_ref, f32[1,1536]{1,0:T(1,128)} %broadcast_in_dim.24.bias_ref, bf16[128,1664]{1,0:T(8,128)(2,1)} %get-tuple-element.55.refs_0_, bf16[128,1664]{1,0:T(8,128)(2,1)} %copy-done.6, ...), custom_call_target="tpu_custom_call" | custom-call | flops 203436112 | bytes 2109524 | tf_op jit(solution)/shard_map/pallas_call | solution.py:239
  79.0 9.7 %shard_map.175 = (bf16[128,4352]{1,0:T(8,128)(2,1)}, bf16[128,1280]{1,0:T(8,128)(2,1)}, f32[1,2048]{1,0:T(1,128)}, bf16[128,512]{1,0:T(8,128)(2,1)}, bf16[128,51...) custom-call(s32[21]{0:T(128)} %get-tuple-element.96.token_ref.core_ref.index_ref, ...), custom_call_target="tpu_custom_call" | custom-call | flops 2830409728 | bytes 11837524 | tf_op jit(solution)/shard_map/pallas_call | solution.py:239
  89.3 2.5 %collective-permute-done.41.refs_3_.refs_1_ = bf16[128,4352]{1,0:T(8,128)(2,1)S(1)} collective-permute-done((bf16[128,4352]{1,0:T(8,128)(2,1)}, bf16[128,4352]{1,0:T(8,128)(2,1)S(1)}, u32[]{:S(2)}, u32[]{:S(2)}) %collective-permute-start.41) | collective-permute-done | bytes 1114144 | tf_op jit(solution)/shard_map/ppermute | solution.py:167
  92.8 3.1 %shard_map.179 = (bf16[128,768]{1,0:T(8,128)(2,1)}, bf16[128,768]{1,0:T(8,128)(2,1)}, bf16[128,768]{1,0:T(8,128)(2,1)}, bf16[128,768]{1,0:T(8,128)(2,1)}, bf16[1...) custom-call(s32[21]{0:T(128)} %get-tuple-element.96.token_ref.core_ref.index, ...), custom_call_target="tpu_custom_call" | custom-call | flops 406782048 | bytes 4128852 | tf_op jit(solution)/shard_map/pallas_call | solution.py:239
  98.5 3.8 %shard_map.176 = (bf16[256,640]{1,0:T(8,128)(2,1)}, bf16[256,640]{1,0:T(8,128)(2,1)}, bf16[256,640]{1,0:T(8,128)(2,1)}, bf16[256,640]{1,0:T(8,128)(2,1)}, bf16[2...) custom-call(s32[21]{0:T(128)} %get-tuple-element.96.token_ref.core_ref.index, ...), custom_call_target="tpu_custom_call" | custom-call | flops 542195776 | bytes 5324884 | tf_op jit(solution)/shard_map/pallas_call | solution.py:239
  106.8 5.5 %collective-permute-done.45 = bf16[256,640]{1,0:T(8,128)(2,1)S(1)} collective-permute-done((bf16[256,640]{1,0:T(8,128)(2,1)}, bf16[256,640]{1,0:T(8,128)(2,1)S(1)}, u32[]{:S(2)}, u32[]{:S(2)}) %collective-permute-start.45) | collective-permute-done | bytes 327712 | tf_op jit(solution)/shard_map/ppermute | solution.py:167
  116.7 3.0 %collective-permute-done.49 = bf16[256,640]{1,0:T(8,128)(2,1)S(1)} collective-permute-done((bf16[256,640]{1,0:T(8,128)(2,1)}, bf16[256,640]{1,0:T(8,128)(2,1)S(1)}, u32[]{:S(2)}, u32[]{:S(2)}) %collective-permute-start.49) | collective-permute-done | bytes 327712 | tf_op jit(solution)/shard_map/ppermute | solution.py:167
  120.3 5.1 %collective-permute-done.46 = bf16[256,640]{1,0:T(8,128)(2,1)S(1)} collective-permute-done((bf16[256,640]{1,0:T(8,128)(2,1)S(1)}, bf16[256,640]{1,0:T(8,128)(2,1)S(1)}, u32[]{:S(2)}, u32[]{:S(2)}) %collective-permute-start.46) | collective-permute-done | bytes 327712 | tf_op jit(solution)/shard_map/ppermute | solution.py:167
  127.7 5.7 %collective-permute-done.50 = bf16[256,640]{1,0:T(8,128)(2,1)S(1)} collective-permute-done((bf16[256,640]{1,0:T(8,128)(2,1)S(1)}, bf16[256,640]{1,0:T(8,128)(2,1)S(1)}, u32[]{:S(2)}, u32[]{:S(2)}) %collective-permute-start.50) | collective-permute-done | bytes 327712 | tf_op jit(solution)/shard_map/ppermute | solution.py:167
  136.2 4.9 %collective-permute-done.59 = bf16[128,768]{1,0:T(8,128)(2,1)S(1)} collective-permute-done((bf16[128,768]{1,0:T(8,128)(2,1)S(1)}, bf16[128,768]{1,0:T(8,128)(2,1)S(1)}, u32[]{:S(2)}, u32[]{:S(2)}) %collective-permute-start.59) | collective-permute-done | bytes 196640 | tf_op jit(solution)/shard_map/ppermute | solution.py:167
  141.2 3.5 %collective-permute-done.51 = bf16[256,640]{1,0:T(8,128)(2,1)S(1)} collective-permute-done((bf16[256,640]{1,0:T(8,128)(2,1)S(1)}, bf16[256,640]{1,0:T(8,128)(2,1)S(1)}, u32[]{:S(2)}, u32[]{:S(2)}) %collective-permute-start.51) | collective-permute-done | bytes 327712 | tf_op jit(solution)/shard_map/ppermute | solution.py:167
  149.0 7.4 %attend_back.1 = (bf16[3,128,512]{2,1,0:T(8,128)(2,1)}, bf16[3,128,512]{2,1,0:T(8,128)(2,1)}, bf16[3,128,512]{2,1,0:T(8,128)(2,1)}, bf16[3,128,512]{2,1,0:T(8,128)(2,1)}) custom-call(bf16[3,128,512]{2,1,0:T(8,128)(2,1)} %get-tuple-element.51.refs_0_, bf16[3,128,512]{2,1,0:T(8,128)(2,1)} %copy-done.26, bf16[3,128,512]{2,1,0:T(8,128)(2,1)} %copy-done.27, ...), custom_call_target="tpu_custom_call" | custom-call | flops 1342177280 | bytes 3670016 | tf_op jit(solution)/shard_map/attend_back/pallas_call | solution.py:124
  159.5 21.3 %collective-permute-done.61 = bf16[128,768]{1,0:T(8,128)(2,1)S(1)} collective-permute-done((bf16[128,768]{1,0:T(8,128)(2,1)S(1)}, bf16[128,768]{1,0:T(8,128)(2,1)S(1)}, u32[]{:S(2)}, u32[]{:S(2)}) %collective-permute-start.61) | collective-permute-done | bytes 196640 | tf_op jit(solution)/shard_map/ppermute | solution.py:167
  182.1 2.6 %shard_map.177 = (bf16[128,2048]{1,0:T(8,128)(2,1)}, bf16[128,2048]{1,0:T(8,128)(2,1)}, bf16[128,2048]{1,0:T(8,128)(2,1)}) custom-call(s32[4]{0:T(128)} %slice_bitcast_fusion.owner_ref, bf16[3,128,512]{2,1,0:T(8,128)(2,1)} %get-tuple-element.72.refs_0_, bf16[3,128,512]{2,1,0:T(8,128)(2,1)} %copy-done.9, bf16[3,128,512]{2,1,0:T(8,128)(2,1)} %copy-done.10, ...), custom_call_target="tpu_custom_call" | custom-call | flops 3145744 | bytes 3145744 | tf_op jit(solution)/shard_map/pallas_call | solution.py:239
  (255 shorter events, 70.1 us)
Async XLA Ops:
  10.6 13.6 %collective-permute-start = (bf16[3,128,512]{2,1,0:T(8,128)(2,1)}, bf16[3,128,512]{2,1,0:T(8,128)(2,1)S(1)}, u32[]{:S(2)}, u32[]{:S(2)}) collective-permute-start(bf16[3,128,512]{2,1,0:T(8,128)(2,1)} %get-tuple-element.52), channel_id=1, source_target_pairs={{0,1},{1,0},{2,3},{3,2},{4,5},{5,4},{6,7},{7,6},{8,9},{9,8},{10,11... | collective-permute-start | bytes 1179656 | tf_op jit(solution)/shard_map/ppermute | solution.py:167
  12.7 12.2 %collective-permute-start.1 = (bf16[3,128,512]{2,1,0:T(8,128)(2,1)}, bf16[3,128,512]{2,1,0:T(8,128)(2,1)S(1)}, u32[]{:S(2)}, u32[]{:S(2)}) collective-permute-start(bf16[3,128,512]{2,1,0:T(8,128)(2,1)} %get-tuple-element.53), channel_id=1, source_target_pairs={{0,2},{1,3},{2,0},{3,1},{4,6},{5,7},{6,4},{7,5},{8,10},{9,11},{10,... | collective-permute-start | bytes 1179656 | tf_op jit(solution)/shard_map/ppermute | solution.py:167
  14.7 18.2 %collective-permute-start.2 = (bf16[3,128,512]{2,1,0:T(8,128)(2,1)}, bf16[3,128,512]{2,1,0:T(8,128)(2,1)S(1)}, u32[]{:S(2)}, u32[]{:S(2)}) collective-permute-start(bf16[3,128,512]{2,1,0:T(8,128)(2,1)} %get-tuple-element.54), channel_id=1, source_target_pairs={{0,3},{1,2},{2,1},{3,0},{4,7},{5,6},{6,5},{7,4},{8,11},{9,10},{10,... | collective-permute-start | bytes 1179656 | tf_op jit(solution)/shard_map/ppermute | solution.py:167
  20.9 22.6 %collective-permute-start.3 = (bf16[128,1664]{1,0:T(8,128)(2,1)}, bf16[128,1664]{1,0:T(8,128)(2,1)S(1)}, u32[]{:S(2)}, u32[]{:S(2)}) collective-permute-start(bf16[128,1664]{1,0:T(8,128)(2,1)} %get-tuple-element.55.refs_0_), channel_id=1, source_target_pairs={{0,2},{1,3},{2,0},{3,1},{4,6},{5,7},{6,4},{7,5},{8,10},{9,11},{10,... | collective-permute-start | bytes 1277960 | tf_op jit(solution)/shard_map/ppermute | solution.py:167
  22.7 10.5 %collective-permute-start.30 = (bf16[128,768]{1,0:T(8,128)(2,1)}, bf16[128,768]{1,0:T(8,128)(2,1)S(1)}, u32[]{:S(2)}, u32[]{:S(2)}) collective-permute-start(bf16[128,768]{1,0:T(8,128)(2,1)} %collective-permute-done.29.refs_34_), channel_id=1, source_target_pairs={{0,4},{1,5},{2,6},{3,7},{4,12},{5,13},{6,14},{7,15},{8,0},{9,1},{1... | collective-permute-start | bytes 589832 | tf_op jit(solution)/shard_map/ppermute | solution.py:167
  24.2 19.8 %collective-permute-start.4 = (bf16[128,1664]{1,0:T(8,128)(2,1)}, bf16[128,1664]{1,0:T(8,128)(2,1)S(1)}, u32[]{:S(2)}, u32[]{:S(2)}) collective-permute-start(bf16[128,1664]{1,0:T(8,128)(2,1)} %get-tuple-element.55.refs_0_), channel_id=1, source_target_pairs={{0,1},{1,0},{2,3},{3,2},{4,5},{5,4},{6,7},{7,6},{8,9},{9,8},{10,11... | collective-permute-start | bytes 1277960 | tf_op jit(solution)/shard_map/ppermute | solution.py:167
  24.9 14.7 %collective-permute-start.25 = (bf16[128,768]{1,0:T(8,128)(2,1)}, bf16[128,768]{1,0:T(8,128)(2,1)S(1)}, u32[]{:S(2)}, u32[]{:S(2)}) collective-permute-start(bf16[128,768]{1,0:T(8,128)(2,1)} %collective-permute-done.23.refs_22_), channel_id=1, source_target_pairs={{0,8},{1,9},{2,10},{3,11},{4,0},{5,1},{6,2},{7,3},{8,16},{9,17},{1... | collective-permute-start | bytes 589832 | tf_op jit(solution)/shard_map/ppermute | solution.py:167
  40.0 14.2 %collective-permute-start.11 = (bf16[256,640]{1,0:T(8,128)(2,1)S(1)}, bf16[256,640]{1,0:T(8,128)(2,1)S(1)}, u32[]{:S(2)}, u32[]{:S(2)}) collective-permute-start(bf16[256,640]{1,0:T(8,128)(2,1)S(1)} %collective-permute-done.9.refs_6_), channel_id=1, source_target_pairs={{0,8},{1,9},{2,10},{3,11},{4,0},{5,1},{6,2},{7,3},{8,16},{9,17},{1... | collective-permute-start | bytes 983048 | tf_op jit(solution)/shard_map/ppermute | solution.py:167
  57.5 12.6 %collective-permute-start.5 = (bf16[128,1664]{1,0:T(8,128)(2,1)S(1)}, bf16[128,1664]{1,0:T(8,128)(2,1)S(1)}, u32[]{:S(2)}, u32[]{:S(2)}) collective-permute-start(bf16[128,1664]{1,0:T(8,128)(2,1)S(1)} %collective-permute-done.3.refs_1_), channel_id=1, source_target_pairs={{0,1},{1,0},{2,3},{3,2},{4,5},{5,4},{6,7},{7,6},{8,9},{9,8},{10,11... | collective-permute-start | bytes 1277960 | tf_op jit(solution)/shard_map/ppermute | solution.py:167
  60.3 13.1 %collective-permute-start.19 = (bf16[256,640]{1,0:T(8,128)(2,1)S(1)}, bf16[256,640]{1,0:T(8,128)(2,1)}, u32[]{:S(2)}, u32[]{:S(2)}) collective-permute-start(bf16[256,640]{1,0:T(8,128)(2,1)S(1)} %collective-permute-done.18.refs_16_), channel_id=1, source_target_pairs={{0,4},{1,5},{2,6},{3,7},{4,12},{5,13},{6,14},{7,15},{8,0},{9,1},{1... | collective-permute-start | bytes 983048 | tf_op jit(solution)/shard_map/ppermute | solution.py:167
  104.0 42.9 %collective-permute-start.37 = (bf16[128,512]{1,0:T(8,128)(2,1)S(1)}, bf16[128,512]{1,0:T(8,128)(2,1)S(1)}, u32[]{:S(2)}, u32[]{:S(2)}) collective-permute-start(bf16[128,512]{1,0:T(8,128)(2,1)S(1)} %copy-done.50), channel_id=1, source_target_pairs={{0,1},{1,0},{2,3},{3,2},{4,5},{5,4},{6,7},{7,6},{8,9},{9,8},{10,11... | collective-permute-start | bytes 393224 | tf_op jit(solution)/shard_map/ppermute | solution.py:167
  104.0 44.3 %collective-permute-start.38 = (bf16[128,512]{1,0:T(8,128)(2,1)S(1)}, bf16[128,512]{1,0:T(8,128)(2,1)S(1)}, u32[]{:S(2)}, u32[]{:S(2)}) collective-permute-start(bf16[128,512]{1,0:T(8,128)(2,1)S(1)} %copy-done.49), channel_id=1, source_target_pairs={{0,2},{1,3},{2,0},{3,1},{4,6},{5,7},{6,4},{7,5},{8,10},{9,11},{10,... | collective-permute-start | bytes 393224 | tf_op jit(solution)/shard_map/ppermute | solution.py:167
  106.2 13.5 %collective-permute-start.49 = (bf16[256,640]{1,0:T(8,128)(2,1)}, bf16[256,640]{1,0:T(8,128)(2,1)S(1)}, u32[]{:S(2)}, u32[]{:S(2)}) collective-permute-start(bf16[256,640]{1,0:T(8,128)(2,1)} %get-tuple-element.83), channel_id=1, source_target_pairs={{0,4},{1,5},{2,6},{3,7},{4,12},{5,13},{6,14},{7,15},{8,0},{9,1},{1... | collective-permute-start | bytes 983048 | tf_op jit(solution)/shard_map/ppermute | solution.py:167
  112.3 23.3 %collective-permute-start.55 = (bf16[128,768]{1,0:T(8,128)(2,1)S(1)}, bf16[128,768]{1,0:T(8,128)(2,1)S(1)}, u32[]{:S(2)}, u32[]{:S(2)}) collective-permute-start(bf16[128,768]{1,0:T(8,128)(2,1)S(1)} %add_convert_fusion.11), channel_id=1, source_target_pairs={{0,8},{1,9},{2,10},{3,11},{4,0},{5,1},{6,2},{7,3},{8,16},{9,17},{1... | collective-permute-start | bytes 589832 | tf_op jit(solution)/shard_map/ppermute | solution.py:167
  133.9 10.8 %collective-permute-start.51 = (bf16[256,640]{1,0:T(8,128)(2,1)S(1)}, bf16[256,640]{1,0:T(8,128)(2,1)S(1)}, u32[]{:S(2)}, u32[]{:S(2)}) collective-permute-start(bf16[256,640]{1,0:T(8,128)(2,1)S(1)} %add_convert_fusion.1), channel_id=1, source_target_pairs={{0,4},{1,5},{2,6},{3,7},{4,12},{5,13},{6,14},{7,15},{8,0},{9,1},{1... | collective-permute-start | bytes 983048 | tf_op jit(solution)/shard_map/ppermute | solution.py:167
  135.6 10.7 %collective-permute-start.48 = (bf16[256,640]{1,0:T(8,128)(2,1)S(1)}, bf16[256,640]{1,0:T(8,128)(2,1)S(1)}, u32[]{:S(2)}, u32[]{:S(2)}) collective-permute-start(bf16[256,640]{1,0:T(8,128)(2,1)S(1)} %add_convert_fusion.3), channel_id=1, source_target_pairs={{0,8},{1,9},{2,10},{3,11},{4,0},{5,1},{6,2},{7,3},{8,16},{9,17},{1... | collective-permute-start | bytes 983048 | tf_op jit(solution)/shard_map/ppermute | solution.py:167
  144.8 12.5 %collective-permute-start.56 = (bf16[128,768]{1,0:T(8,128)(2,1)S(1)}, bf16[128,768]{1,0:T(8,128)(2,1)S(1)}, u32[]{:S(2)}, u32[]{:S(2)}) collective-permute-start(bf16[128,768]{1,0:T(8,128)(2,1)S(1)} %add_convert_fusion.10), channel_id=1, source_target_pairs={{0,8},{1,9},{2,10},{3,11},{4,0},{5,1},{6,2},{7,3},{8,16},{9,17},{1... | collective-permute-start | bytes 589832 | tf_op jit(solution)/shard_map/ppermute | solution.py:167
  146.3 12.0 %collective-permute-start.60 = (bf16[128,768]{1,0:T(8,128)(2,1)S(1)}, bf16[128,768]{1,0:T(8,128)(2,1)S(1)}, u32[]{:S(2)}, u32[]{:S(2)}) collective-permute-start(bf16[128,768]{1,0:T(8,128)(2,1)S(1)} %add_convert_fusion.7), channel_id=1, source_target_pairs={{0,4},{1,5},{2,6},{3,7},{4,12},{5,13},{6,14},{7,15},{8,0},{9,1},{1... | collective-permute-start | bytes 589832 | tf_op jit(solution)/shard_map/ppermute | solution.py:167
  146.9 12.3 %collective-permute-start.52 = (bf16[256,640]{1,0:T(8,128)(2,1)S(1)}, bf16[256,640]{1,0:T(8,128)(2,1)S(1)}, u32[]{:S(2)}, u32[]{:S(2)}) collective-permute-start(bf16[256,640]{1,0:T(8,128)(2,1)S(1)} %fusion), channel_id=1, source_target_pairs={{0,2},{1,3},{2,0},{3,1},{4,6},{5,7},{6,4},{7,5},{8,10},{9,11},{10,... | collective-permute-start | bytes 983048 | tf_op jit(solution)/shard_map/ppermute | solution.py:167
  156.4 24.6 %collective-permute-start.42 = (bf16[3,128,512]{2,1,0:T(8,128)(2,1)}, bf16[3,128,512]{2,1,0:T(8,128)(2,1)S(1)}, u32[]{:S(2)}, u32[]{:S(2)}) collective-permute-start(bf16[3,128,512]{2,1,0:T(8,128)(2,1)} %get-tuple-element.73), channel_id=1, source_target_pairs={{0,1},{1,0},{2,3},{3,2},{4,5},{5,4},{6,7},{7,6},{8,9},{9,8},{10,11... | collective-permute-start | bytes 1179656 | tf_op jit(solution)/shard_map/ppermute | solution.py:167
  156.5 24.6 %collective-permute-start.43 = (bf16[3,128,512]{2,1,0:T(8,128)(2,1)}, bf16[3,128,512]{2,1,0:T(8,128)(2,1)S(1)}, u32[]{:S(2)}, u32[]{:S(2)}) collective-permute-start(bf16[3,128,512]{2,1,0:T(8,128)(2,1)} %get-tuple-element.74), channel_id=1, source_target_pairs={{0,2},{1,3},{2,0},{3,1},{4,6},{5,7},{6,4},{7,5},{8,10},{9,11},{10,... | collective-permute-start | bytes 1179656 | tf_op jit(solution)/shard_map/ppermute | solution.py:167
  157.3 23.8 %collective-permute-start.44 = (bf16[3,128,512]{2,1,0:T(8,128)(2,1)}, bf16[3,128,512]{2,1,0:T(8,128)(2,1)S(1)}, u32[]{:S(2)}, u32[]{:S(2)}) collective-permute-start(bf16[3,128,512]{2,1,0:T(8,128)(2,1)} %get-tuple-element.75), channel_id=1, source_target_pairs={{0,3},{1,2},{2,1},{3,0},{4,7},{5,6},{6,5},{7,4},{8,11},{9,10},{10,... | collective-permute-start | bytes 1179656 | tf_op jit(solution)/shard_map/ppermute | solution.py:167
  158.5 22.4 %collective-permute-start.61 = (bf16[128,768]{1,0:T(8,128)(2,1)S(1)}, bf16[128,768]{1,0:T(8,128)(2,1)S(1)}, u32[]{:S(2)}, u32[]{:S(2)}) collective-permute-start(bf16[128,768]{1,0:T(8,128)(2,1)S(1)} %fusion.1), channel_id=1, source_target_pairs={{0,2},{1,3},{2,0},{3,1},{4,6},{5,7},{6,4},{7,5},{8,10},{9,11},{10,... | collective-permute-start | bytes 589832 | tf_op jit(solution)/shard_map/ppermute | solution.py:167
  159.4 28.0 %collective-permute-start.53 = (bf16[256,640]{1,0:T(8,128)(2,1)S(1)}, bf16[256,640]{1,0:T(8,128)(2,1)S(1)}, u32[]{:S(2)}, u32[]{:S(2)}) collective-permute-start(bf16[256,640]{1,0:T(8,128)(2,1)S(1)} %add_convert_fusion.refs_0_), channel_id=1, source_target_pairs={{0,1},{1,0},{2,3},{3,2},{4,5},{5,4},{6,7},{7,6},{8,9},{9,8},{10,11... | collective-permute-start | bytes 983048 | tf_op jit(solution)/shard_map/ppermute | solution.py:167
  (95 other events, 979.8 us)
